TPU v7x, 32 devices: a whole 2x2x4 slice. The times are simulated.
32 devices in a mesh: bank: 4 (over y, x), zero: 8 (over z, core).
Axes of the slice: x: 2, y: 2, z: 4, core: 2. Of those that a mesh axis runs over, the one named last changes fastest.
Arguments:
- w_down: float32 [64, 1024, 2048], P('bank', None, 'zero'), may hold values from -0.25 to 0.25
- avg_down: bfloat16 [64, 1024, 2048], P('bank', None, 'zero'), may hold values from -0.09375 to 0.09375
- router_weight: float32 [2048, 64], P('zero', 'bank'), may hold values from -0.125 to 0.125
- router_gain: float32 [2048], P('zero'), may hold values from 0.25 to 1.75
Outputs:
- serve_down: bfloat16 [64, 1024, 2048], P('bank')
- scale_down: float32 [64, 1024], P('bank')
- serve_router: bfloat16 [2048, 64], replicated
All inputs are finite; a program needn't handle non-finite values.
Results may differ from a plain program's by a relative error of at most 0.001.
Values may be sent and summed in bfloat16 or wider, within the bound.
A program may use at most 256 MiB of HBM per device.

v0:
```python
import jax
import jax.numpy as jnp
from jax import lax
from jax.sharding import PartitionSpec as P


def shards(w_down, avg_down, router_weight, router_gain):
    fresh_down = w_down + avg_down.astype(jnp.float32)
    total_down = lax.psum(jnp.sum(fresh_down * fresh_down, axis=2), "zero")
    scale_down = jnp.sqrt(total_down)
    narrow_down = (fresh_down / jnp.expand_dims(scale_down, 2)).astype(jnp.bfloat16)
    serve_down = lax.all_gather(narrow_down, "zero", axis=2, tiled=True)
    part_router = (router_weight * router_gain[:, None]).astype(jnp.bfloat16)
    row_router = lax.all_gather(part_router, "zero", axis=0, tiled=True)
    serve_router = lax.all_gather(row_router, "bank", axis=1, tiled=True)
    return (serve_down, scale_down, serve_router)


def solution(mesh):
    return jax.shard_map(
        shards,
        mesh=mesh,
        in_specs=(P("bank", None, "zero"), P("bank", None, "zero"), P("zero", "bank"), P("zero")),
        out_specs=(P("bank", None, None), P("bank", None), P()),
        check_vma=False,
    )
```

profile of v0, /device:TPU:0, one launch (start us, length us, event | category | flops | bytes accessed | tf_op | source)
XLA Modules:
  0.0 706.3 jit_solution(10193368544461576350)
XLA Ops:
  7.2 0.0 all-reduce.2.cloned.1.call-start
  7.2 9.7 %multiply_reduce_fusion = f32[16,1024]{1,0:T(8,128)} fusion(f32[16,1024,256]{2,1,0:T(8,128)} %param.4, bf16[16,1024,256]{2,1,0:T(8,128)(2,1)} %param.5), kind=kLoop, calls=%fused_computation.1 | loop fusion | flops 16760832 | bytes 25231360 | tf_op jit(solution)/shard_map/reduce_sum | solution.py:9
  17.0 0.0 all-reduce.2.cloned.1.call-update
  17.0 0.0 all-gather.2.cloned.1.call-start
  17.0 57.5 %all-reduce.2.cloned.1.call-done = f32[16,1024]{1,0:T(8,128)} async-done(((f32[16,1024]{1,0:T(8,128)}), f32[16,1024]{1,0:T(8,128)}) %all-reduce.2.cloned.1.call-update) | async-done | bytes 65552 | tf_op jit(solution)/shard_map/psum | solution.py:9
  74.6 0.9 sqrt.3
  75.4 0.0 copy-start
  75.4 0.0 copy-start.1
  75.4 0.0 copy-start.2
  75.5 12.0 %divide_convert_fusion = bf16[16,1024,256]{2,1,0:T(8,128)(2,1)} fusion(f32[16,1024,256]{2,1,0:T(8,128)} %param.4, bf16[16,1024,256]{2,1,0:T(8,128)(2,1)} %param.5, f32[16,1024]{1,0:T(8,128)S(1)} %sqrt.3), kind=kLoop, calls=%fused_computation | loop fusion | flops 16777216 | bytes 33619968 | tf_op jit(solution)/shard_map/convert_element_type | solution.py:11
  87.5 0.0 copy-done
  87.5 0.0 all-gather.2.cloned.1.call-update
  87.5 0.0 copy-done.1
  87.5 0.0 copy-done.2
  87.5 14.0 %all_gather.10 = bf16[2048,16]{0,1:T(8,128)(2,1)S(1)} all-gather(bf16[256,16]{0,1:T(8,128)(2,1)S(1)} %multiply_convert_fusion), channel_id=1, replica_groups=mesh['bank'=4,'zero'=8] {'zero'}, dimensions={0}, use_global_device_ids=true | all-gather | bytes 73728 | tf_op jit(solution)/shard_map/all_gather | solution.py:14
  101.5 8.9 %all_gather.11 = bf16[2048,64]{0,1:T(8,128)(2,1)S(1)} all-gather(bf16[2048,16]{0,1:T(8,128)(2,1)S(1)} %all_gather.10), channel_id=1, replica_groups=mesh['bank'=4,'zero'=8] {'bank'}, dimensions={1}, use_global_device_ids=true | all-gather | bytes 327680 | tf_op jit(solution)/shard_map/all_gather | solution.py:15
  110.4 544.3 %all-gather.2.cloned.1.call-done = bf16[16,1024,2048]{2,1,0:T(8,128)(2,1)} async-done(((bf16[16,1024,256]{2,1,0:T(8,128)(2,1)}), bf16[16,1024,2048]{2,1,0:T(8,128)(2,1)}) %all-gather.2.cloned.1.call-update) | async-done | bytes 67108880 | tf_op jit(solution)/shard_map/all_gather | solution.py:12
  654.8 44.0 %copy.10 = bf16[16,1024,2048]{2,1,0:T(8,128)(2,1)} copy(bf16[16,1024,2048]{2,1,0:T(8,128)(2,1)} %all-gather.2.cloned.1.call-done) | data formatting | bytes 134217728
  698.8 0.7 copy.11
  (1 shorter events, 0.0 us)
Async XLA Ops:
  7.2 67.4 %all-reduce.2.cloned.1.call-start = ((), (), s32[]{:S(2)}) async-start(), calls=%async_computation | async-start | bytes 131072 | tf_op jit(solution)/shard_map/psum | solution.py:9
  17.0 637.8 %all-gather.2.cloned.1.call-start = ((), (), s32[]{:S(2)}) async-start(), calls=%async_computation.1 | async-start | bytes 75497472 | tf_op jit(solution)/shard_map/all_gather | solution.py:12
  75.4 12.1 %copy-start = (f32[16,1024]{1,0:T(8,128)}, f32[16,1024]{1,0:T(8,128)S(1)}, u32[]{:S(2)}) copy-start(f32[16,1024]{1,0:T(8,128)S(1)} %sqrt.3) | copy-start | bytes 196612
  75.4 12.1 %copy-start.1 = (f32[256,16]{0,1:T(8,128)S(1)}, f32[256,16]{0,1:T(8,128)}, u32[]{:S(2)}) copy-start(f32[256,16]{0,1:T(8,128)} %param.6) | copy-start | bytes 49156
  75.4 12.1 %copy-start.2 = (f32[256]{0:T(256)S(1)}, f32[256]{0:T(256)}, u32[]{:S(2)}) copy-start(f32[256]{0:T(256)} %param.7) | copy-start | bytes 3076
Sparse Core Ops, SparseCore 0:
  17.1 57.4 all-reduce.1
  87.6 567.0 all-gather.1
where the time goes:
time: 708 us; the launch traced here: 706 us
  waiting for transfers between devices  602 us (85%)
  local copies, waits for them, and re-layouts  45.6 us (6%)
  blocking collectives  22.9 us (3%)
  other arithmetic  21.8 us (3%)
  between operations  14.1 us (2%)
    all_gather x1, waiting for transfers between devices, shards(): serve_down = lax.all_gather(narrow_down, 'zero', axis=2, tiled=True)  544 us
    psum x1, waiting for transfers between devices, shards(): total_down = lax.psum(jnp.sum(fresh_down * fresh_down, axis=2), 'zero')  57.5 us
    unnamed x8, local copies, waits for them, and re-layouts  44.8 us
  transfers between devices with their start and end apart: 2, of which 2 were waited for; matrix products, arithmetic and copies ran while one was open for 0% of the time, Pallas kernels for 0%

commit v1 on v0

v1 whole, which is shorter than its diff:
```python
import functools

import jax
import jax.numpy as jnp
from jax import lax
from jax.experimental import pallas as pl
from jax.experimental.pallas import tpu as pltpu
from jax.sharding import PartitionSpec as P

MESH = pl.DeviceIdType.MESH


def exchange_kernel(n, part_ref, out_ref, held, send_sems, recv_sems):
    bank, me = lax.axis_index("bank"), lax.axis_index("zero")
    barrier = pltpu.get_barrier_semaphore()
    for k in range(1, n):
        pl.semaphore_signal(barrier, inc=1, device_id=(bank, lax.rem(me + k, n)), device_id_type=MESH)
    pl.semaphore_wait(barrier, n - 1)
    copies = []
    for k in range(1, n):
        copy = pltpu.make_async_remote_copy(
            src_ref=part_ref,
            dst_ref=held.at[k - 1],
            send_sem=send_sems.at[k - 1],
            recv_sem=recv_sems.at[k - 1],
            device_id=(bank, lax.rem(me + k, n)),
            device_id_type=MESH,
        )
        copy.start()
        copies.append(copy)
    for copy in copies:
        copy.wait()
    total = jnp.zeros(part_ref.shape, jnp.float32)
    for d in range(n):
        slot = lax.rem(me - d + n, n)
        other = held[jnp.maximum(slot - 1, 0)]
        total += jnp.where(slot == 0, part_ref[...], other)
    out_ref[...] = total


def exchange(part, n, cid):
    rows = part.shape
    return pl.pallas_call(
        functools.partial(exchange_kernel, n),
        out_shape=jax.ShapeDtypeStruct(rows, jnp.float32),
        in_specs=[pl.BlockSpec(memory_space=pltpu.VMEM)],
        out_specs=pl.BlockSpec(memory_space=pltpu.VMEM),
        scratch_shapes=[
            pltpu.VMEM((n - 1,) + rows, jnp.float32),
            pltpu.SemaphoreType.DMA((n - 1,)),
            pltpu.SemaphoreType.DMA((n - 1,)),
        ],
        compiler_params=pltpu.CompilerParams(collective_id=cid, has_side_effects=True),
        cost_estimate=pl.CostEstimate(flops=1000, bytes_accessed=20_000_000, transcendentals=0),
        name=f"exchange_{cid}",
    )(part)


def place_kernel(src_ref, *refs):
    refs[-1][...] = src_ref[0]


def place(gathered, base, start, shape):
    n, rows, cols = gathered.shape
    block = 256
    while rows % block or start % block:
        block //= 2
    for bigger in (2048, 1024, 512):
        if rows % bigger == 0 and start % bigger == 0:
            block = bigger
            break
    operands, specs, aliases = [gathered], [pl.BlockSpec((1, block, cols), lambda r, d: (d, r, 0))], {}
    if base is not None:
        operands.append(base)
        specs.append(pl.BlockSpec(memory_space=pl.ANY))
        aliases = {1: 0}
    first = start // block
    return pl.pallas_call(
        place_kernel,
        grid=(rows // block, n),
        out_shape=jax.ShapeDtypeStruct(shape, gathered.dtype),
        in_specs=specs,
        out_specs=pl.BlockSpec((block, cols), lambda r, d: (first + r, d)),
        input_output_aliases=aliases,
        cost_estimate=pl.CostEstimate(flops=0, bytes_accessed=4 * gathered.size, transcendentals=0),
        name=f"place_{start}",
    )(*operands)


def shards(n, w_down, avg_down, router_weight, router_gain):
    experts, inner, cols = w_down.shape
    rows = experts * inner
    w = w_down.reshape(rows, cols)
    a = avg_down.reshape(rows, cols)
    edge = rows // 16
    cuts = [0, edge, rows - edge, rows]

    def sums(w, a, cid):
        fresh = w + a.astype(jnp.float32)
        part = jnp.sum(fresh * fresh, axis=1).reshape(-1, 128)
        return jnp.sqrt(exchange(part, n, cid)).reshape(-1)

    def narrow(w, a, scale):
        return ((w + a.astype(jnp.float32)) / scale[:, None]).astype(jnp.bfloat16)

    def gather(x):
        return lax.all_gather(x, "zero", axis=0)

    scale_0 = sums(w[:edge], a[:edge], 0)
    narrow_0 = narrow(w[:edge], a[:edge], scale_0)
    narrow_0, w, a, router_weight = lax.optimization_barrier((narrow_0, w, a, router_weight))
    gathered_0 = gather(narrow_0)
    scale_1 = sums(w[edge:], a[edge:], 1)
    mid = rows - 2 * edge
    narrow_1 = narrow(w[edge:-edge], a[edge:-edge], scale_1[:mid])
    narrow_2 = narrow(w[-edge:], a[-edge:], scale_1[mid:])
    gathered_1 = gather(narrow_1)
    gathered_2 = gather(narrow_2)
    shape = (rows, cols * n)
    out = place(gathered_0, None, 0, shape)
    out = place(gathered_1, out, edge, shape)
    out = place(gathered_2, out, rows - edge, shape)
    serve_down = out.reshape(experts, inner, cols * n)
    scale_down = jnp.concatenate([scale_0, scale_1]).reshape(experts, inner)
    part_router = (router_weight * router_gain[:, None]).astype(jnp.bfloat16)
    row_router = lax.all_gather(part_router, "zero", axis=0, tiled=True)
    serve_router = lax.all_gather(row_router, "bank", axis=1, tiled=True)
    return (serve_down, scale_down, serve_router)


def solution(mesh):
    return jax.shard_map(
        functools.partial(shards, mesh.shape["zero"]),
        mesh=mesh,
        in_specs=(P("bank", None, "zero"), P("bank", None, "zero"), P("zero", "bank"), P("zero")),
        out_specs=(P("bank", None, None), P("bank", None), P()),
        check_vma=False,
    )
```

time: 708 us -> 667 us (0.942)
  waiting for transfers between devices: 602 us -> 470 us
  Pallas kernels: 0 us -> 118 us
  local copies, waits for them, and re-layouts: 45.6 us -> 2.91 us
  blocking collectives: 22.9 us -> 30.3 us
    pallas_call x0 -> x5, Pallas kernels: none -> 118 us  [the longest x3 88.1 us: place(): pl.pallas_call(place_kernel, grid=(rows // block, n), out_shape=jax.Shape...]
    all_gather x1 -> x3, waiting for transfers between devices: 544 us -> 470 us  [gather(): return lax.all_gather(x, 'zero', axis=0)]
    psum x1 -> x0, waiting for transfers between devices: 57.5 us -> none  [shards(): total_down = lax.psum(jnp.sum(fresh_down * fresh_down, axis=2), 'zero')]
    unnamed x8 -> x5, local copies, waits for them, and re-layouts: 44.8 us -> 0.71 us
    all_gather x1, blocking collectives: 14 us -> 21.2 us  [shards(): row_router = lax.all_gather(part_router, 'zero', axis=0, tiled=True)]
    convert_element_type x1 -> x3, other arithmetic: 12 us -> 17.3 us  [narrow(): return ((w + a.astype(jnp.float32)) / scale[:, None]).astype(jnp.bfloat16)]
  transfers between devices with their start and end apart: 2 -> 3, of which waited for: 2 -> 1; matrix products, arithmetic and copies ran while one was open for 0% -> 4% of each run, Pallas kernels for 0% -> 16%
where the time goes in v1:
time: 667 us; the launch traced here: 664 us
  waiting for transfers between devices  470 us (70%)
  Pallas kernels  118 us (18%)
  blocking collectives  30.3 us (5%)
  other arithmetic  28.8 us (4%)
  between operations  13.8 us (2%)
    all_gather x3, waiting for transfers between devices, gather(): return lax.all_gather(x, 'zero', axis=0)  470 us
    pallas_call x3, Pallas kernels, place(): pl.pallas_call(place_kernel, grid=(rows // block, n), out_shape=jax.Shape...  88.1 us
    pallas_call x2, Pallas kernels, exchange(): pl.pallas_call(functools.partial(exchange_kernel, n), out_shape=jax.Shape...  30.4 us
    all_gather x1, blocking collectives, shards(): row_router = lax.all_gather(part_router, 'zero', axis=0, tiled=True)  21.2 us
    convert_element_type x3, other arithmetic, narrow(): return ((w + a.astype(jnp.float32)) / scale[:, None]).astype(jnp.bfloat16)  17.3 us
  transfers between devices with their start and end apart: 3, of which 1 were waited for; matrix products, arithmetic and copies ran while one was open for 4% of the time, Pallas kernels for 16%

profile of v1, /device:TPU:0, one launch (start us, length us, event | category | flops | bytes accessed | tf_op | source)
XLA Modules:
  0.0 664.0 jit_solution(15308121465095921592)
XLA Ops:
  7.2 0.0 all-gather.11.cloned.1.call-start
  7.2 2.2 fusion
  9.4 8.7 %exchange_0.1 = f32[8,128]{1,0:T(8,128)} custom-call(f32[8,128]{1,0:T(8,128)} %bitcast.33), custom_call_target="tpu_custom_call" | custom-call | flops 1000 | bytes 20000000 | tf_op jit(solution)/shard_map/exchange_0/pallas_call | solution.py:43
  18.1 0.7 sqrt_bitcast_fusion
  18.8 2.4 fusion.1
  21.2 0.0 all-gather.11.cloned.1.call-update
  21.2 0.0 all-gather.9.cloned.1.call-start
  21.2 9.3 %multiply_reduce_fusion = f32[15360]{0:T(1024)} fusion(f32[16384,256]{1,0:T(8,128)} %bitcast.23, bf16[16384,256]{1,0:T(8,128)(2,1)} %bitcast.27), kind=kLoop, calls=%fused_computation | loop fusion | flops 15713280 | bytes 23654400 | tf_op jit(solution)/shard_map/reduce_sum | solution.py:100
  30.5 21.7 %exchange_1.1 = f32[120,128]{1,0:T(8,128)} custom-call(f32[120,128]{1,0:T(8,128)} %bitcast.32), custom_call_target="tpu_custom_call" | custom-call | flops 1000 | bytes 20000000 | tf_op jit(solution)/shard_map/exchange_1/pallas_call | solution.py:43
  52.2 0.8 sqrt_bitcast_fusion.1
  53.1 0.0 copy-start
  53.1 0.0 copy-start.1
  53.1 12.6 %divide_convert_fusion = bf16[14336,256]{1,0:T(8,128)(2,1)} fusion(f32[16384,256]{1,0:T(8,128)} %bitcast.24, f32[14336]{0:T(1024)S(1)} %slice_bitcast_fusion, bf16[16384,256]{1,0:T(8,128)(2,1)} %bitcast.28), kind=kLoop, calls=%fused_computation.1 | loop fusion | flops 14680064 | bytes 29417472 | tf_op jit(solution)/shard_map/convert_element_type | solution.py:104
  65.6 0.0 all-gather.9.cloned.1.call-update
  65.7 0.0 all-gather.7.cloned.1.call-start
  65.7 2.4 divide_convert_fusion.1
  68.1 0.0 all-gather.7.cloned.1.call-update
  68.1 0.6 reshape.46
  68.8 0.0 copy-done
  68.8 0.0 copy-done.1
  68.8 21.2 %all_gather.30 = bf16[2048,16]{0,1:T(8,128)(2,1)S(1)} all-gather(bf16[256,16]{0,1:T(8,128)(2,1)S(1)} %multiply_convert_fusion), channel_id=1, replica_groups=mesh['bank'=4,'zero'=8] {'zero'}, dimensions={0}, use_global_device_ids=true | all-gather | bytes 73728 | tf_op jit(solution)/shard_map/all_gather | solution.py:126
  90.0 9.1 %all_gather.31 = bf16[2048,64]{0,1:T(8,128)(2,1)S(1)} all-gather(bf16[2048,16]{0,1:T(8,128)(2,1)S(1)} %all_gather.30), channel_id=1, replica_groups=mesh['bank'=4,'zero'=8] {'bank'}, dimensions={1}, use_global_device_ids=true | all-gather | bytes 327680 | tf_op jit(solution)/shard_map/all_gather | solution.py:127
  99.1 0.0 all-gather.11.cloned.1.call-done
  99.1 7.0 %place_0.1.refs_0_ = bf16[16384,2048]{1,0:T(8,128)(2,1)} custom-call(bf16[8,1024,256]{2,1,0:T(8,128)(2,1)} %bitcast.30), custom_call_target="tpu_custom_call" | custom-call | bytes 8388608 | tf_op jit(solution)/shard_map/place_0/pallas_call | solution.py:78
  106.1 469.6 %all-gather.9.cloned.1.call-done = bf16[114688,256]{1,0:T(8,128)(2,1)} async-done(((bf16[14336,256]{1,0:T(8,128)(2,1)}), bf16[114688,256]{1,0:T(8,128)(2,1)}) %all-gather.9.cloned.1.call-update) | async-done | bytes 58720272 | tf_op jit(solution)/shard_map/all_gather | solution.py:107
  575.7 74.6 %place_1024.1.refs_0_ = bf16[16384,2048]{1,0:T(8,128)(2,1)} custom-call(bf16[8,14336,256]{2,1,0:T(8,128)(2,1)} %bitcast.26, bf16[16384,2048]{1,0:T(8,128)(2,1)} %place_0.1.refs_0_), custom_call_target="tpu_custom_call", output_to_operand_aliasing={{}: (1, {})} | custom-call | bytes 117440512 | tf_op jit(solution)/shard_map/place_1024/pallas_call | solution.py:78
  650.2 0.0 all-gather.7.cloned.1.call-done
  650.2 6.6 place_15360.1
  656.8 0.7 copy.12
  (4 shorter events, 0.0 us)
Async XLA Ops:
  7.2 92.0 %all-gather.11.cloned.1.call-start = ((), (), s32[]{:S(2)}) async-start(), calls=%async_computation.2 | async-start | bytes 4718592 | tf_op jit(solution)/shard_map/all_gather | solution.py:107
  21.2 554.5 %all-gather.9.cloned.1.call-start = ((), (), s32[]{:S(2)}) async-start(), calls=%async_computation.1 | async-start | bytes 66060288 | tf_op jit(solution)/shard_map/all_gather | solution.py:107
  53.1 15.7 %copy-start = (f32[256,16]{0,1:T(8,128)S(1)}, f32[256,16]{0,1:T(8,128)}, u32[]{:S(2)}) copy-start(f32[256,16]{0,1:T(8,128)} %param.6) | copy-start | bytes 49156
  53.1 15.7 %copy-start.1 = (f32[256]{0:T(256)S(1)}, f32[256]{0:T(256)}, u32[]{:S(2)}) copy-start(f32[256]{0:T(256)} %param.7) | copy-start | bytes 3076
  65.7 584.6 %all-gather.7.cloned.1.call-start = ((), (), s32[]{:S(2)}) async-start(), calls=%async_computation | async-start | bytes 4718592 | tf_op jit(solution)/shard_map/all_gather | solution.py:107
Sparse Core Ops, SparseCore 0:
  21.3 58.4 all-gather.10
  81.4 494.2 all-gather.8
  577.3 45.0 all-gather.6

commit v2 on v1

--- a/solution.py
+++ b/solution.py
@@ -56,31 +56,94 @@
     )(part)
 
 
-def place_kernel(src_ref, *refs):
-    refs[-1][...] = src_ref[0]
+def exchange_two_kernel(n, part_ref, out_ref, held, own, gathered, send_sems, recv_sems, send_sems_2, recv_sems_2):
+    bank, me = lax.axis_index("bank"), lax.axis_index("zero")
+    barrier = pltpu.get_barrier_semaphore()
+    for k in range(1, n):
+        pl.semaphore_signal(barrier, inc=1, device_id=(bank, lax.rem(me + k, n)), device_id_type=MESH)
+    pl.semaphore_wait(barrier, n - 1)
+    scatter = []
+    for k in range(1, n):
+        peer = lax.rem(me + k, n)
+        copy = pltpu.make_async_remote_copy(
+            src_ref=part_ref.at[peer],
+            dst_ref=held.at[k - 1],
+            send_sem=send_sems.at[k - 1],
+            recv_sem=recv_sems.at[k - 1],
+            device_id=(bank, peer),
+            device_id_type=MESH,
+        )
+        copy.start()
+        scatter.append(copy)
+    total = part_ref[me]
+    for k in range(1, n):
+        scatter[k - 1].wait_recv()
+        total += held[k - 1]
+    own[...] = total
+    out_ref[me] = total
+    for copy in scatter:
+        copy.wait_send()
+    spread = []
+    for k in range(1, n):
+        copy = pltpu.make_async_remote_copy(
+            src_ref=own,
+            dst_ref=gathered.at[k - 1],
+            send_sem=send_sems_2.at[k - 1],
+            recv_sem=recv_sems_2.at[k - 1],
+            device_id=(bank, lax.rem(me + k, n)),
+            device_id_type=MESH,
+        )
+        copy.start()
+        spread.append(copy)
+    for k in range(1, n):
+        spread[k - 1].wait_recv()
+        out_ref[lax.rem(me - k + n, n)] = gathered[k - 1]
+    for copy in spread:
+        copy.wait_send()
+
+
+def exchange_two(part, n, cid):
+    block = (part.shape[0] // n,) + part.shape[1:]
+    return pl.pallas_call(
+        functools.partial(exchange_two_kernel, n),
+        out_shape=jax.ShapeDtypeStruct((n,) + block, jnp.float32),
+        in_specs=[pl.BlockSpec(memory_space=pltpu.VMEM)],
+        out_specs=pl.BlockSpec(memory_space=pltpu.VMEM),
+        scratch_shapes=[
+            pltpu.VMEM((n - 1,) + block, jnp.float32),
+            pltpu.VMEM(block, jnp.float32),
+            pltpu.VMEM((n - 1,) + block, jnp.float32),
+        ]
+        + [pltpu.SemaphoreType.DMA((n - 1,))] * 4,
+        compiler_params=pltpu.CompilerParams(collective_id=cid, has_side_effects=True),
+        cost_estimate=pl.CostEstimate(flops=1000, bytes_accessed=20_000_000, transcendentals=0),
+        name=f"exchange_{cid}",
+    )(part.reshape((n,) + block)).reshape(part.shape)
+
+
+def place_kernel(n, src_ref, *refs):
+    cols = src_ref.shape[2]
+    for d in range(n):
+        refs[-1][:, d * cols : (d + 1) * cols] = src_ref[d]
 
 
 def place(gathered, base, start, shape):
     n, rows, cols = gathered.shape
-    block = 256
+    block = 512 if rows > 1024 else 256
     while rows % block or start % block:
         block //= 2
-    for bigger in (2048, 1024, 512):
-        if rows % bigger == 0 and start % bigger == 0:
-            block = bigger
-            break
-    operands, specs, aliases = [gathered], [pl.BlockSpec((1, block, cols), lambda r, d: (d, r, 0))], {}
+    operands, specs, aliases = [gathered], [pl.BlockSpec((n, block, cols), lambda r: (0, r, 0))], {}
     if base is not None:
         operands.append(base)
         specs.append(pl.BlockSpec(memory_space=pl.ANY))
         aliases = {1: 0}
     first = start // block
     return pl.pallas_call(
-        place_kernel,
-        grid=(rows // block, n),
+        functools.partial(place_kernel, n),
+        grid=(rows // block,),
         out_shape=jax.ShapeDtypeStruct(shape, gathered.dtype),
         in_specs=specs,
-        out_specs=pl.BlockSpec((block, cols), lambda r, d: (first + r, d)),
+        out_specs=pl.BlockSpec((block, n * cols), lambda r: (first + r, 0)),
         input_output_aliases=aliases,
         cost_estimate=pl.CostEstimate(flops=0, bytes_accessed=4 * gathered.size, transcendentals=0),
         name=f"place_{start}",
@@ -93,12 +156,11 @@
     w = w_down.reshape(rows, cols)
     a = avg_down.reshape(rows, cols)
     edge = rows // 16
-    cuts = [0, edge, rows - edge, rows]
 
-    def sums(w, a, cid):
+    def sums(w, a, cid, how):
         fresh = w + a.astype(jnp.float32)
         part = jnp.sum(fresh * fresh, axis=1).reshape(-1, 128)
-        return jnp.sqrt(exchange(part, n, cid)).reshape(-1)
+        return jnp.sqrt(how(part, n, cid)).reshape(-1)
 
     def narrow(w, a, scale):
         return ((w + a.astype(jnp.float32)) / scale[:, None]).astype(jnp.bfloat16)
@@ -106,14 +168,13 @@
     def gather(x):
         return lax.all_gather(x, "zero", axis=0)
 
-    scale_0 = sums(w[:edge], a[:edge], 0)
+    scale_0 = sums(w[:edge], a[:edge], 0, exchange)
     narrow_0 = narrow(w[:edge], a[:edge], scale_0)
     narrow_0, w, a, router_weight = lax.optimization_barrier((narrow_0, w, a, router_weight))
     gathered_0 = gather(narrow_0)
-    scale_1 = sums(w[edge:], a[edge:], 1)
-    mid = rows - 2 * edge
-    narrow_1 = narrow(w[edge:-edge], a[edge:-edge], scale_1[:mid])
-    narrow_2 = narrow(w[-edge:], a[-edge:], scale_1[mid:])
+    scale = sums(w, a, 1, exchange_two)
+    narrow_1 = narrow(w[edge:-edge], a[edge:-edge], scale[edge:-edge])
+    narrow_2 = narrow(w[-edge:], a[-edge:], scale[-edge:])
     gathered_1 = gather(narrow_1)
     gathered_2 = gather(narrow_2)
     shape = (rows, cols * n)
@@ -121,7 +182,7 @@
     out = place(gathered_1, out, edge, shape)
     out = place(gathered_2, out, rows - edge, shape)
     serve_down = out.reshape(experts, inner, cols * n)
-    scale_down = jnp.concatenate([scale_0, scale_1]).reshape(experts, inner)
+    scale_down = scale.reshape(experts, inner)
     part_router = (router_weight * router_gain[:, None]).astype(jnp.bfloat16)
     row_router = lax.all_gather(part_router, "zero", axis=0, tiled=True)
     serve_router = lax.all_gather(row_router, "bank", axis=1, tiled=True)

time: 667 us -> 630 us (0.945)
  Pallas kernels: 118 us -> 82.3 us
  waiting for transfers between devices: 470 us -> 478 us
  blocking collectives: 30.3 us -> 23 us
    pallas_call x2 -> x1, Pallas kernels: 30.4 us -> 8.72 us  [exchange(): pl.pallas_call(functools.partial(exchange_kernel, n), out_shape=jax.Shape...]
    pallas_call x3 -> x4, Pallas kernels: 88.1 us -> 73.6 us  [the longest x3 59.3 us: place(): pl.pallas_call(functools.partial(place_kernel, n), grid=(rows // block,),...]
    all_gather x3, waiting for transfers between devices: 470 us -> 478 us  [gather(): return lax.all_gather(x, 'zero', axis=0)]
    all_gather x1, blocking collectives: 21.2 us -> 14.1 us  [shards(): row_router = lax.all_gather(part_router, 'zero', axis=0, tiled=True)]
  transfers between devices with their start and end apart: 3 -> 3, of which waited for: 1 -> 1; matrix products, arithmetic and copies ran while one was open for 4% -> 4% of each run, Pallas kernels for 16% -> 11%
where the time goes in v2:
time: 630 us; the launch traced here: 629 us
  waiting for transfers between devices  478 us (76%)
  Pallas kernels  82.3 us (13%)
  other arithmetic  29.5 us (5%)
  blocking collectives  23 us (4%)
  between operations  13.8 us (2%)
    all_gather x3, waiting for transfers between devices, gather(): return lax.all_gather(x, 'zero', axis=0)  478 us
    pallas_call x3, Pallas kernels, place(): pl.pallas_call(functools.partial(place_kernel, n), grid=(rows // block,),...  59.3 us
    convert_element_type x3, other arithmetic, narrow(): return ((w + a.astype(jnp.float32)) / scale[:, None]).astype(jnp.bfloat16)  17.4 us
    pallas_call x1, Pallas kernels, exchange_two(): pl.pallas_call(functools.partial(exchange_two_kernel, n), out_shape=jax.S...  14.3 us
    all_gather x1, blocking collectives, shards(): row_router = lax.all_gather(part_router, 'zero', axis=0, tiled=True)  14.1 us
  transfers between devices with their start and end apart: 3, of which 1 were waited for; matrix products, arithmetic and copies ran while one was open for 4% of the time, Pallas kernels for 11%

profile of v2, /device:TPU:0, one launch (start us, length us, event | category | flops | bytes accessed | tf_op | source)
XLA Modules:
  0.0 629.4 jit_solution(6596406649064361082)
XLA Ops:
  7.2 0.0 all-gather.11.cloned.1.call-start
  7.2 2.2 fusion
  9.4 8.7 %exchange_0.1 = f32[8,128]{1,0:T(8,128)} custom-call(f32[8,128]{1,0:T(8,128)} %bitcast.34), custom_call_target="tpu_custom_call" | custom-call | flops 1000 | bytes 20000000 | tf_op jit(solution)/shard_map/exchange_0/pallas_call | solution.py:43
  18.1 0.7 sqrt_bitcast_fusion
  18.8 2.4 fusion.1
  21.2 0.0 all-gather.11.cloned.1.call-update
  21.2 0.0 all-gather.9.cloned.1.call-start
  21.2 9.9 %multiply_reduce_fusion = f32[16384]{0:T(1024)} fusion(f32[16384,256]{1,0:T(8,128)} %bitcast.22, bf16[16384,256]{1,0:T(8,128)(2,1)} %bitcast.26), kind=kLoop, calls=%fused_computation | loop fusion | flops 16760832 | bytes 25231360 | tf_op jit(solution)/shard_map/reduce_sum | solution.py:162
  31.1 14.3 %exchange_1.1 = f32[8,16,128]{2,1,0:T(8,128)} custom-call(f32[8,16,128]{2,1,0:T(8,128)} %bitcast.33), custom_call_target="tpu_custom_call" | custom-call | flops 1000 | bytes 20000000 | tf_op jit(solution)/shard_map/exchange_1/pallas_call | solution.py:107
  45.4 0.9 sqrt.14
  46.3 0.0 copy-start
  46.3 0.0 copy-start.1
  46.3 12.7 %divide_convert_fusion = bf16[14336,256]{1,0:T(8,128)(2,1)} fusion(f32[16384,256]{1,0:T(8,128)} %bitcast.23, f32[14336]{0:T(1024)S(1)} %slice_bitcast_fusion, bf16[16384,256]{1,0:T(8,128)(2,1)} %bitcast.27), kind=kLoop, calls=%fused_computation.1 | loop fusion | flops 14680064 | bytes 29417472 | tf_op jit(solution)/shard_map/convert_element_type | solution.py:166
  59.0 0.0 all-gather.9.cloned.1.call-update
  59.0 0.0 all-gather.7.cloned.1.call-start
  59.1 2.4 divide_convert_fusion.1
  61.5 0.0 all-gather.7.cloned.1.call-update
  61.5 0.6 sqrt.16
  62.1 0.0 copy-done
  62.1 0.0 copy-done.1
  62.1 14.1 %all_gather.30 = bf16[2048,16]{0,1:T(8,128)(2,1)S(1)} all-gather(bf16[256,16]{0,1:T(8,128)(2,1)S(1)} %multiply_convert_fusion), channel_id=1, replica_groups=mesh['bank'=4,'zero'=8] {'zero'}, dimensions={0}, use_global_device_ids=true | all-gather | bytes 73728 | tf_op jit(solution)/shard_map/all_gather | solution.py:187
  76.3 8.9 %all_gather.31 = bf16[2048,64]{0,1:T(8,128)(2,1)S(1)} all-gather(bf16[2048,16]{0,1:T(8,128)(2,1)S(1)} %all_gather.30), channel_id=1, replica_groups=mesh['bank'=4,'zero'=8] {'bank'}, dimensions={1}, use_global_device_ids=true | all-gather | bytes 327680 | tf_op jit(solution)/shard_map/all_gather | solution.py:188
  85.1 0.0 all-gather.11.cloned.1.call-done
  85.1 5.3 place_0.1.refs_0_
  90.5 477.7 %all-gather.9.cloned.1.call-done = bf16[114688,256]{1,0:T(8,128)(2,1)} async-done(((bf16[14336,256]{1,0:T(8,128)(2,1)}), bf16[114688,256]{1,0:T(8,128)(2,1)}) %all-gather.9.cloned.1.call-update) | async-done | bytes 58720272 | tf_op jit(solution)/shard_map/all_gather | solution.py:169
  568.1 49.2 %place_1024.1.refs_0_ = bf16[16384,2048]{1,0:T(8,128)(2,1)} custom-call(bf16[8,14336,256]{2,1,0:T(8,128)(2,1)} %bitcast.25, bf16[16384,2048]{1,0:T(8,128)(2,1)} %place_0.1.refs_0_), custom_call_target="tpu_custom_call", output_to_operand_aliasing={{}: (1, {})} | custom-call | bytes 117440512 | tf_op jit(solution)/shard_map/place_1024/pallas_call | solution.py:141
  617.3 0.0 all-gather.7.cloned.1.call-done
  617.3 4.8 place_15360.1
  622.1 0.7 copy.12
  (3 shorter events, 0.0 us)
Async XLA Ops:
  7.2 78.0 %all-gather.11.cloned.1.call-start = ((), (), s32[]{:S(2)}) async-start(), calls=%async_computation.2 | async-start | bytes 4718592 | tf_op jit(solution)/shard_map/all_gather | solution.py:169
  21.2 546.9 %all-gather.9.cloned.1.call-start = ((), (), s32[]{:S(2)}) async-start(), calls=%async_computation.1 | async-start | bytes 66060288 | tf_op jit(solution)/shard_map/all_gather | solution.py:169
  46.3 15.9 %copy-start = (f32[256,16]{0,1:T(8,128)S(1)}, f32[256,16]{0,1:T(8,128)}, u32[]{:S(2)}) copy-start(f32[256,16]{0,1:T(8,128)} %param.6) | copy-start | bytes 49156
  46.3 15.8 %copy-start.1 = (f32[256]{0:T(256)S(1)}, f32[256]{0:T(256)}, u32[]{:S(2)}) copy-start(f32[256]{0:T(256)} %param.7) | copy-start | bytes 3076
  59.0 558.3 %all-gather.7.cloned.1.call-start = ((), (), s32[]{:S(2)}) async-start(), calls=%async_computation | async-start | bytes 4718592 | tf_op jit(solution)/shard_map/all_gather | solution.py:169
Sparse Core Ops, SparseCore 0:
  21.3 50.9 all-gather.10
  74.0 494.1 all-gather.8
  569.7 45.0 all-gather.6
